TPU v7x, 32 devices: a whole 2x2x4 slice. The times are simulated.
32 devices in a mesh: replica: 4 (over z), tensor: 8 (over y, x, core).
Axes of the slice: x: 2, y: 2, z: 4, core: 2. Of those that a mesh axis runs over, the one named last changes fastest.
Arguments:
- hidden_in: bfloat16 [4, 64, 8192], P(None, 'replica'), may hold values from -96 to 96
- norm_gain: bfloat16 [8192], replicated, may hold values from 0.25 to 1.75
- query_weight: bfloat16 [8192, 8192], P(None, 'tensor'), may hold values from -0.0625 to 0.0625
- w_keyvalue: bfloat16 [8192, 2048], P(None, 'tensor'), may hold values from -0.0625 to 0.0625
- output_weight: bfloat16 [8192, 8192], P('tensor'), may hold values from -0.0625 to 0.0625
- query_down_factor: bfloat16 [64, 8192], P(None, ('replica', 'tensor')), may hold values from -0.0625 to 0.0625
- query_up_factor: bfloat16 [64, 8192], P(None, ('replica', 'tensor')), may hold values from -0.75 to 0.75
- output_down_factor: bfloat16 [64, 8192], P(None, ('replica', 'tensor')), may hold values from -0.0625 to 0.0625
- output_up_factor: bfloat16 [64, 8192], P(None, ('replica', 'tensor')), may hold values from -0.75 to 0.75
- keys_cache: bfloat16 [16, 32, 1024, 128], P('tensor', 'replica'), may hold values from -250 to 250
- values_cache: bfloat16 [16, 32, 1024, 128], P('tensor', 'replica'), may hold values from -5 to 5
- cache_lengths: int32 [64], P('replica'), may hold values from 256 to 1024, as said below
Outputs:
- attended: bfloat16 [4, 64, 8192], P(None, 'replica', 'tensor')
Inputs may be any that keep to these rules, and one draw needn't show every extreme that they name: `cache_lengths`: some row holds exactly 1024 positions and some other row exactly 256.
All inputs are finite; a program needn't handle non-finite values.
Results may differ from a plain program's by a relative error of at most 0.018.
Values may be sent and summed in bfloat16 or wider, within the bound.
No kernel may reach another device: no remote copies, remote signals or barrier semaphores. Data moves between devices by JAX's collectives and lax.ppermute only.
A program may use at most 128 MiB of HBM per device.

v0:
```python
import math
import jax
import jax.numpy as jnp
from jax import lax
from jax.sharding import PartitionSpec as P

HQ = 64
KVH = 8
HD = 128
CAP = 1024
adapter_scale = 2.0
rope_base = 1000000.0
norm_epsilon = 1e-06


def swapped(array, axis, apart):
    return lax.ppermute(array, axis, [(i, i ^ 1 << apart) for i in range(lax.axis_size(axis))])


def for_sending(array):
    return jax.tree.map(lambda a: a.astype(jnp.bfloat16) if a.dtype == jnp.float32 else a, array)


def rms_norm(hidden, norm_gain):
    values = hidden.astype(jnp.float32)
    mean_square = jnp.mean(values * values, axis=-1, keepdims=True)
    return values * lax.rsqrt(mean_square + norm_epsilon) * norm_gain.astype(jnp.float32)


def apply_rotary(vectors, positions):
    half_width = vectors.shape[-1] // 2
    exponents = jnp.arange(half_width, dtype=jnp.float32) * (2.0 / vectors.shape[-1])
    frequency = jnp.power(rope_base, -exponents)
    angles = positions.astype(jnp.float32)[:, None, None] * frequency
    cosine_values = jnp.cos(angles)
    sine_values = jnp.sin(angles)
    leading = vectors[..., :half_width]
    trailing = vectors[..., half_width:]
    return jnp.concatenate(
        [
            leading * cosine_values - trailing * sine_values,
            trailing * cosine_values + leading * sine_values,
        ],
        axis=-1,
    )


def attend_block(queries, cache_keys, cache_values, lengths, fresh_keys, fresh_values):
    inverse_root = 1.0 / math.sqrt(queries.shape[-1])
    cached = (
        jnp.einsum("ngd,npd->ngp", queries, cache_keys, preferred_element_type=jnp.float32)
        * inverse_root
    )
    visible = jnp.arange(cache_keys.shape[1])[None, :] < lengths[:, None]
    cached = jnp.where(visible[:, None, :], cached, -jnp.inf)
    recent = (
        jnp.einsum("ngd,nsd->ngs", queries, fresh_keys, preferred_element_type=jnp.float32)
        * inverse_root
    )
    highest = jnp.maximum(
        jnp.max(cached, axis=-1, keepdims=True), jnp.max(recent, axis=-1, keepdims=True)
    )
    cached_exp = jnp.exp(cached - highest)
    recent_exp = jnp.exp(recent - highest)
    denominator = jnp.sum(cached_exp, axis=-1, keepdims=True) + jnp.sum(
        recent_exp, axis=-1, keepdims=True
    )
    cached_weight = (cached_exp / denominator).astype(jnp.bfloat16)
    recent_weight = (recent_exp / denominator).astype(jnp.bfloat16)
    combined = jnp.einsum(
        "ngp,npd->ngd", cached_weight, cache_values, preferred_element_type=jnp.float32
    )
    combined = combined + jnp.einsum(
        "ngs,nsd->ngd", recent_weight, fresh_values, preferred_element_type=jnp.float32
    )
    return combined.astype(jnp.bfloat16)


def rank_contraction(left_factor, right_factor):
    return lax.dot_general(
        left_factor, right_factor, (((0,), (0,)), ((), ())), preferred_element_type=jnp.float32
    )


def pick_half(paired, lower_half):
    return jnp.where(lower_half, paired[:, 0], paired[:, 1])


def pick_middle(paired, lower_half):
    return jnp.where(lower_half, paired[:, :, 0], paired[:, :, 1])


def shards(
    hidden_in,
    norm_gain,
    query_weight,
    w_keyvalue,
    output_weight,
    query_down_factor,
    query_up_factor,
    output_down_factor,
    output_up_factor,
    keys_cache,
    values_cache,
    cache_lengths,
):
    tensor_index = lax.axis_index("tensor")
    slice_width = query_weight.shape[1]
    complete_down_factor, complete_up_factor, wide_up, wide_down = (
        lax.all_gather(query_down_factor, ("replica", "tensor"), axis=1, tiled=True),
        lax.all_gather(output_up_factor, ("replica", "tensor"), axis=1, tiled=True),
        lax.all_gather(query_up_factor, ("replica", "tensor"), axis=1, tiled=True),
        lax.all_gather(output_down_factor, ("replica", "tensor"), axis=1, tiled=True),
    )
    query_weight_slice = lax.dynamic_slice_in_dim(
        wide_up, tensor_index * slice_width, slice_width, 1
    )
    output_weight_slice = lax.dynamic_slice_in_dim(
        wide_down, tensor_index * slice_width, slice_width, 1
    )
    query_merged_weight = (
        query_weight.astype(jnp.float32)
        + adapter_scale * rank_contraction(complete_down_factor, query_weight_slice)
    ).astype(jnp.bfloat16)
    output_merged_weight = (
        output_weight.astype(jnp.float32)
        + adapter_scale * rank_contraction(output_weight_slice, complete_up_factor)
    ).astype(jnp.bfloat16)
    rows_local = hidden_in.shape[1]
    rows_half = rows_local // 2
    heads_local = slice_width // HD
    group_size = HQ // KVH
    entries = keys_cache.shape[0]
    lower_half = tensor_index % 2 == 0
    groups_local = max(heads_local // group_size, 1)
    block_count = groups_local * 2 * rows_half
    if entries == 1:
        own_lengths = pick_half(cache_lengths.reshape(rows_half, 2), lower_half)
        own_keys = keys_cache[0]
        own_values = values_cache[0]
    else:
        own_lengths = jnp.tile(cache_lengths.reshape(rows_half, 2).T, (groups_local, 1)).reshape(
            block_count
        )
        own_keys = keys_cache.reshape(block_count, CAP, HD)
        own_values = values_cache.reshape(block_count, CAP, HD)
    step_count = hidden_in.shape[0]
    normed_all = (
        rms_norm(hidden_in, norm_gain)
        .astype(jnp.bfloat16)
        .reshape(step_count * rows_local, hidden_in.shape[2])
    )
    positions_all = (
        cache_lengths[None, :] + jnp.arange(step_count, dtype=jnp.int32)[:, None]
    ).reshape(step_count * rows_local)
    queries_all = jnp.dot(
        normed_all, query_merged_weight, preferred_element_type=jnp.float32
    ).reshape(step_count * rows_local, heads_local, HD)
    queries_all = apply_rotary(queries_all, positions_all).astype(jnp.bfloat16)
    projected_all = jnp.dot(normed_all, w_keyvalue, preferred_element_type=jnp.float32)
    heads_list = []
    if entries == 1:
        rotated_all = apply_rotary(projected_all[:, None, :], positions_all)[:, 0]
        projected_all = jnp.where(lower_half, rotated_all, projected_all).astype(jnp.bfloat16)
        query_pairs = queries_all.reshape(step_count, rows_half, 2, heads_local, HD)
        projected_pairs = projected_all.reshape(step_count, rows_half, 2, HD)
        own_queries = pick_middle(query_pairs, lower_half)
        other_queries = pick_middle(query_pairs, jnp.logical_not(lower_half))
        own_projected = pick_middle(projected_pairs, lower_half)
        other_projected = pick_middle(projected_pairs, jnp.logical_not(lower_half))
        outgoing = jnp.concatenate(
            [other_queries.reshape(step_count, rows_half, heads_local * HD), other_projected],
            axis=2,
        )
        incoming = swapped(outgoing, "tensor", 0)
        partner_queries = incoming[:, :, : heads_local * HD].reshape(
            step_count, rows_half, heads_local, HD
        )
        partner_projected = incoming[:, :, heads_local * HD :]
        group_queries_all = jnp.where(
            lower_half,
            jnp.concatenate([own_queries, partner_queries], axis=2),
            jnp.concatenate([partner_queries, own_queries], axis=2),
        )
        keys_steps = jnp.where(lower_half, own_projected, partner_projected).transpose(1, 0, 2)
        values_steps = jnp.where(lower_half, partner_projected, own_projected).transpose(1, 0, 2)
        kept_list = []
        sent_list = []
        for decode_step in range(step_count):
            attended_heads = attend_block(
                group_queries_all[decode_step],
                own_keys,
                own_values,
                own_lengths,
                keys_steps[:, : decode_step + 1],
                values_steps[:, : decode_step + 1],
            )
            first_heads = attended_heads[:, :heads_local]
            second_heads = attended_heads[:, heads_local:]
            kept_list.append(
                jnp.where(lower_half, first_heads, second_heads).reshape(
                    rows_half, heads_local * HD
                )
            )
            sent_list.append(
                jnp.where(lower_half, second_heads, first_heads).reshape(
                    rows_half, heads_local * HD
                )
            )
        kept_all = jnp.stack(kept_list)
        returned_all = swapped(for_sending(jnp.stack(sent_list)), "tensor", 0)
        rows_first = jnp.where(lower_half, kept_all, returned_all)
        rows_second = jnp.where(lower_half, returned_all, kept_all)
        heads_stacked = jnp.stack([rows_first, rows_second], axis=2).reshape(
            step_count * rows_local, heads_local * HD
        )
    else:
        keyvals = projected_all.reshape(step_count, rows_local, groups_local, 2, HD)
        new_keys = apply_rotary(
            keyvals[:, :, :, 0].reshape(step_count * rows_local, groups_local, HD), positions_all
        ).astype(jnp.bfloat16)
        new_values = keyvals[:, :, :, 1].astype(jnp.bfloat16)
        keys_steps = (
            new_keys.reshape(step_count, rows_half, 2, groups_local, HD)
            .transpose(3, 2, 1, 0, 4)
            .reshape(block_count, step_count, HD)
        )
        values_steps = (
            new_values.reshape(step_count, rows_half, 2, groups_local, HD)
            .transpose(3, 2, 1, 0, 4)
            .reshape(block_count, step_count, HD)
        )
        group_queries_all = (
            queries_all.reshape(step_count, rows_half, 2, groups_local, group_size, HD)
            .transpose(0, 3, 2, 1, 4, 5)
            .reshape(step_count, block_count, group_size, HD)
        )
        for decode_step in range(step_count):
            attended_heads = attend_block(
                group_queries_all[decode_step],
                own_keys,
                own_values,
                own_lengths,
                keys_steps[:, : decode_step + 1],
                values_steps[:, : decode_step + 1],
            )
            heads_list.append(
                attended_heads.reshape(groups_local, 2, rows_half, group_size, HD)
                .transpose(2, 1, 0, 3, 4)
                .reshape(rows_local, heads_local * HD)
            )
        heads_stacked = jnp.stack(heads_list).reshape(step_count * rows_local, heads_local * HD)
    partial_all = jnp.dot(heads_stacked, output_merged_weight, preferred_element_type=jnp.float32)
    shares_all = lax.psum_scatter(
        partial_all.astype(jnp.bfloat16), "tensor", scatter_dimension=1, tiled=True
    ).astype(jnp.float32)
    return shares_all.reshape(step_count, rows_local, shares_all.shape[1]).astype(jnp.bfloat16)


def solution(mesh):
    return jax.shard_map(
        shards,
        mesh=mesh,
        in_specs=(
            P(None, "replica", None),
            P(),
            P(None, "tensor"),
            P(None, "tensor"),
            P("tensor", None),
            P(None, ("replica", "tensor")),
            P(None, ("replica", "tensor")),
            P(None, ("replica", "tensor")),
            P(None, ("replica", "tensor")),
            P("tensor", "replica", None, None),
            P("tensor", "replica", None, None),
            P("replica"),
        ),
        out_specs=P(None, "replica", "tensor"),
        check_vma=False,
    )
```

profile of v0, /device:TPU:0, one launch (start us, length us, event | category | flops | bytes accessed | tf_op | source)
XLA Modules:
  0.0 284.2 jit_solution(3601060914490597169)
XLA Ops:
  6.5 0.7 all-gather.5.cloned.1.call-update
  7.3 0.7 all-gather.7.cloned.1.call-update
  8.1 0.7 all-gather.11.cloned.1.call-update
  8.8 0.5 all-gather.9.cloned.1.call-update
  9.4 0.7 add_convert_fusion.5
  10.0 0.7 reshape.366
  10.8 0.7 convert_element_type.109
  11.5 1.5 fusion.6
  13.0 6.5 %copy.40 = bf16[256,8192]{1,0:T(8,128)(2,1)} copy(bf16[256,8192]{0,1:T(8,128)(2,1)} %bitcast.116) | data formatting | bytes 8388608 | tf_op jit(solution)/shard_map/reshape.133
  19.5 0.3 fusion.8
  19.8 4.0 %convolution_bitcast_fusion = f32[4,16,1,2,128]{4,1,3,0,2:T(8,128)S(1)} fusion(bf16[2,128,8192,1]{2,1,0,3:T(8,128)(2,1)} %bitcast.117, bf16[4,16,8192]{2,1,0:T(8,128)(2,1)S(1)} %fusion.8), kind=kOutput, calls=%fused_computation.23 | convolution fusion | flops 268435456 | bytes 5308416 | tf_op jit(solution)/shard_map/dot_general | solution.py:160
  23.9 20.9 %copy.24 = bf16[8192,1024]{0,1:T(8,128)(2,1)} copy(bf16[8192,1024]{1,0:T(8,128)(2,1)} %param.14) | data formatting | bytes 33554432 | tf_op args[2]
  44.8 0.1 convert_element_type.114
  44.9 0.2 multiply_cosine_fusion.1
  45.1 0.2 fusion.41
  45.4 0.1 lt.15
  45.5 0.1 iota_compare_fusion
  45.6 0.1 pad_maximum_fusion.1
  45.7 19.6 %all-gather.5.cloned.1.call-done = bf16[64,8192]{1,0:T(8,128)(2,1)} async-done(((bf16[64,256]{1,0:T(8,128)(2,1)}), bf16[64,8192]{1,0:T(8,128)(2,1)}) %all-gather.5.cloned.1.call-update) | async-done | bytes 1048592 | tf_op jit(solution)/shard_map/all_gather | solution.py:112
  65.3 54.9 %all-gather.7.cloned.1.call-done = bf16[64,8192]{1,0:T(8,128)(2,1)} async-done(((bf16[64,256]{1,0:T(8,128)(2,1)}), bf16[64,8192]{1,0:T(8,128)(2,1)}) %all-gather.7.cloned.1.call-update) | async-done | bytes 1048592 | tf_op jit(solution)/shard_map/all_gather | solution.py:110
  120.1 11.8 %fusion = bf16[8192,1024]{0,1:T(8,128)(2,1)} fusion(bf16[8192,1024]{0,1:T(8,128)(2,1)} %copy.24, bf16[64,8192]{1,0:T(8,128)(2,1)} %all-gather.7.cloned.1.call-done, bf16[64,8192]{1,0:T(8,128)(2,1)} %all-gather.5.cloned.1.call-done, s32[]{:T(128)S(6)} %select_n.17), kind=kOutput, calls=%fused_computation.1 | convolution fusion | flops 1107296256 | bytes 34734084 | tf_op jit(solution)/shard_map/dot_general | solution.py:80
  131.9 9.3 %fusion.72 = f32[64,8,128]{2,0,1:T(8,128)S(1)} fusion(bf16[64,8192,1]{1,0,2:T(8,128)(2,1)} %bitcast.115, bf16[8,128,8192]{2,1,0:T(8,128)(2,1)} %bitcast.106), kind=kOutput, calls=%fused_computation.122 | convolution fusion | flops 1073741824 | bytes 18087936 | tf_op jit(solution)/shard_map/dot_general | solution.py:156
  141.2 0.1 subtract_convert_fusion
  141.4 0.4 maximum_bitcast_fusion
  141.7 0.1 fusion.64
  141.9 0.1 fusion.57
  142.0 0.2 fusion.70
  142.2 1.3 fusion.71
  143.4 2.0 fusion.69
  145.5 0.2 fusion.68
  145.6 1.3 fusion.67
  146.9 0.2 fusion.18
  147.2 0.7 fusion.16
  148.0 0.2 fusion.19
  148.2 2.9 %fusion.22 = f32[16,8,128]{2,1,0:T(8,128)S(1)} fusion(bf16[16,1024,128]{2,1,0:T(8,128)(2,1)} %bitcast.111, f32[16,8,1024]{2,1,0:T(8,128)S(1)} %copy-done.3, f32[16,8]{1,0:T(8,128)S(1)} %add.101, f32[16,8]{1,0:T(8,128)S(1)} %max.31), kind=kOutput, calls=%fused_computation.45 | convolution fusion | flops 33947648 | bytes 4785152 | tf_op jit(solution)/shard_map/ngp,npd->ngd/dot_general | solution.py:70
  151.1 0.2 fusion.13
  151.4 0.2 fusion.20
  151.7 2.9 %fusion.23 = f32[16,8,128]{2,1,0:T(8,128)S(1)} fusion(bf16[16,1024,128]{2,1,0:T(8,128)(2,1)} %bitcast.112, f32[16,8,1024]{2,1,0:T(8,128)S(1)} %get-tuple-element.22, f32[16,8]{1,0:T(8,128)S(1)} %add.103, f32[16,8]{1,0:T(8,128)S(1)} %max.32), kind=kOutput, calls=%fused_computation.46 | convolution fusion | flops 33947648 | bytes 4785152 | tf_op jit(solution)/shard_map/ngp,npd->ngd/dot_general | solution.py:70
  154.6 0.2 fusion.14
  154.9 0.2 fusion.66
  155.1 3.6 %fusion.65 = (f32[16,8]{1,0:T(8,128)S(1)}, f32[16,8,1024]{2,1,0:T(8,128)S(1)}) fusion(bf16[16,8,128]{2,1,0:T(8,128)(2,1)S(1)} %bitcast.121, bf16[16,1024,128]{2,1,0:T(8,128)(2,1)} %bitcast.107, pred[16,1024]{1,0:T(8,128)(4,1)S(1)} %iota_compare_fusion), kind=kOutput, calls=%fused_computation.115 | convolution fusion | flops 33947520 | bytes 4768256 | tf_op jit(solution)/shard_map/ngd,npd->ngp/dot_general | solution.py:51
  158.7 0.2 fusion.21
  159.0 0.7 fusion.24
  159.7 0.2 fusion.15
  160.0 15.2 %all-gather.11.cloned.1.call-done = bf16[64,8192]{1,0:T(8,128)(2,1)} async-done(((bf16[64,256]{1,0:T(8,128)(2,1)}), bf16[64,8192]{1,0:T(8,128)(2,1)}) %all-gather.11.cloned.1.call-update) | async-done | bytes 1048592 | tf_op jit(solution)/shard_map/all_gather | solution.py:111
  175.1 54.7 %all-gather.9.cloned.1.call-done = bf16[64,8192]{1,0:T(8,128)(2,1)} async-done(((bf16[64,256]{1,0:T(8,128)(2,1)}), bf16[64,8192]{1,0:T(8,128)(2,1)}) %all-gather.9.cloned.1.call-update) | async-done | bytes 1048592 | tf_op jit(solution)/shard_map/all_gather | solution.py:113
  229.9 12.0 %fusion.5 = bf16[64,8192]{1,0:T(8,128)(2,1)} fusion(bf16[64,1024]{1,0:T(8,128)(2,1)S(1)} %bitcast.130, bf16[1024,8192]{1,0:T(8,128)(2,1)} %param.16, bf16[64,8192]{1,0:T(8,128)(2,1)} %all-gather.11.cloned.1.call-done, bf16[64,8192]{1,0:T(8,128)(2,1)} %all-gather.9.cloned.1.call-done, s32[]{:T(128)S(6)} %select_n.17), kind=kOutput, calls=%fused_computation.6 | convolution fusion | flops 2181562368 | bytes 19136516 | tf_op jit(solution)/shard_map/dot_general | solution.py:253
  241.9 35.8 %reduce-scatter.2.cloned.1.call-done = bf16[64,1024]{1,0:T(8,128)(2,1)} async-done(((bf16[64,8192]{1,0:T(8,128)(2,1)}), bf16[64,1024]{1,0:T(8,128)(2,1)}) %reduce-scatter.2.cloned.1.call-update) | async-done | bytes 131088 | tf_op jit(solution)/shard_map/reduce_scatter | solution.py:254
  (51 shorter events, 0.7 us)
Async XLA Ops:
  6.5 58.7 %all-gather.5.cloned.1.call-start = ((), (), s32[]{:S(2)}) async-start(), calls=%async_computation.1 | async-start | bytes 1081344 | tf_op jit(solution)/shard_map/all_gather | solution.py:112
  7.3 112.9 %all-gather.7.cloned.1.call-start = ((), (), s32[]{:S(2)}) async-start(), calls=%async_computation.2 | async-start | bytes 1081344 | tf_op jit(solution)/shard_map/all_gather | solution.py:110
  8.0 167.1 %all-gather.11.cloned.1.call-start = ((), (), s32[]{:S(2)}) async-start(), calls=%async_computation.4 | async-start | bytes 1081344 | tf_op jit(solution)/shard_map/all_gather | solution.py:111
  8.7 221.2 %all-gather.9.cloned.1.call-start = ((), (), s32[]{:S(2)}) async-start(), calls=%async_computation.3 | async-start | bytes 1081344 | tf_op jit(solution)/shard_map/all_gather | solution.py:113
  9.3 268.4 %reduce-scatter.2.cloned.1.call-start = ((), (), s32[]{:S(2)}) async-start(), calls=%async_computation.5 | async-start | bytes 1179648 | tf_op jit(solution)/shard_map/reduce_scatter | solution.py:254
  13.0 6.5 %copy-start.5 = (bf16[4,16,8192]{2,1,0:T(8,128)(2,1)S(1)}, bf16[4,16,8192]{2,1,0:T(8,128)(2,1)}, u32[]{:S(2)}) copy-start(bf16[4,16,8192]{2,1,0:T(8,128)(2,1)} %param.12) | copy-start | bytes 3145732
  19.8 25.0 %copy-start.4 = (bf16[4,16,8192]{2,1,0:T(8,128)(2,1)}, bf16[4,16,8192]{2,1,0:T(8,128)(2,1)S(1)}, u32[]{:S(2)}) copy-start(bf16[4,16,8192]{2,1,0:T(8,128)(2,1)S(1)} %fusion.8) | copy-start | bytes 3145732
  131.9 10.3 %copy-start = (bf16[2,8,1024,128]{3,2,1,0:T(8,128)(2,1)S(1)}, bf16[2,8,1024,128]{3,2,1,0:T(8,128)(2,1)}, u32[]{:S(2)}) copy-start(bf16[2,8,1024,128]{3,2,1,0:T(8,128)(2,1)} %param.21) | copy-start | bytes 12582916
  143.4 3.7 %copy-start.1 = (bf16[2,8,1024,128]{3,2,1,0:T(8,128)(2,1)S(1)}, bf16[2,8,1024,128]{3,2,1,0:T(8,128)(2,1)}, u32[]{:S(2)}) copy-start(bf16[2,8,1024,128]{3,2,1,0:T(8,128)(2,1)} %param.22) | copy-start | bytes 12582916
  146.9 1.1 copy-start.3
  154.9 4.1 %copy-start.2 = (bf16[2,8,1024,128]{3,2,1,0:T(8,128)(2,1)S(1)}, bf16[2,8,1024,128]{3,2,1,0:T(8,128)(2,1)}, u32[]{:S(2)}) copy-start(bf16[2,8,1024,128]{3,2,1,0:T(8,128)(2,1)} %param.22) | copy-start | bytes 12582916
Sparse Core Ops, SparseCore 0:
  10.2 55.0 all-gather.4
  68.1 51.9 all-gather.6
  123.0 52.0 all-gather.10
  177.9 51.9 all-gather.8
  242.0 35.6 reduce-scatter.1
where the time goes:
time: 285 us; the launch traced here: 284 us
  waiting for transfers between devices  183 us (64%)
  matrix products  53.7 us (19%)
  local copies, waits for them, and re-layouts  28.7 us (10%)
  between operations  13.5 us (5%)
  other arithmetic  5.41 us (2%)
    all_gather x1, waiting for transfers between devices, shards(): lax.all_gather(query_down_factor, ('replica', 'tensor'), axis=1, tiled=True)  54.9 us
    all_gather x1, waiting for transfers between devices, shards(): lax.all_gather(output_down_factor, ('replica', 'tensor'), axis=1, tiled=T...  54.7 us
    reduce_scatter x1, waiting for transfers between devices, shards(): lax.psum_scatter(partial_all.astype(jnp.bfloat16), 'tensor', scatter_dime...  35.8 us
    unnamed x13, local copies, waits for them, and re-layouts  21 us
    all_gather x1, waiting for transfers between devices, shards(): lax.all_gather(query_up_factor, ('replica', 'tensor'), axis=1, tiled=True)  19.6 us
    all_gather x1, waiting for transfers between devices, shards(): lax.all_gather(output_up_factor, ('replica', 'tensor'), axis=1, tiled=True)  15.2 us
    dot_general x1, matrix products, shards(): jnp.dot(heads_stacked, output_merged_weight, preferred_element_type=jnp.f...  12 us
    dot_general x1, matrix products, rank_contraction(): lax.dot_general(left_factor, right_factor, (((0,), (0,)), ((), ())), pref...  11.8 us
  transfers between devices with their start and end apart: 5, of which 5 were waited for; matrix products, arithmetic and copies ran while one was open for 27% of the time, Pallas kernels for 0%

commit v1 on v0

--- a/solution.py
+++ b/solution.py
@@ -3,6 +3,7 @@
 import jax.numpy as jnp
 from jax import lax
 from jax.sharding import PartitionSpec as P
+from jax.lax import axis_index, axis_size, ppermute
 
 HQ = 64
 KVH = 8
@@ -11,6 +12,19 @@
 adapter_scale = 2.0
 rope_base = 1000000.0
 norm_epsilon = 1e-06
+
+
+def read_the_signs(vals, mesh_dim):
+    b_now = axis_size(mesh_dim)
+    everything = axis_index(mesh_dim)
+    t1, long_array, val = (b_now, everything, vals.shape[1])
+    small, low = (vals, 1)
+    while low < t1:
+        placed = tuple(((rr, (rr - low) % t1) for rr in range(t1)))
+        right_arr = ppermute(small, mesh_dim, placed)
+        small = jnp.concatenate([small, right_arr], axis=1)
+        low = 2 * low
+    return jnp.roll(small, long_array * val, 1)
 
 
 def swapped(array, axis, apart):
@@ -109,7 +123,7 @@
     complete_down_factor, complete_up_factor, wide_up, wide_down = (
         lax.all_gather(query_down_factor, ("replica", "tensor"), axis=1, tiled=True),
         lax.all_gather(output_up_factor, ("replica", "tensor"), axis=1, tiled=True),
-        lax.all_gather(query_up_factor, ("replica", "tensor"), axis=1, tiled=True),
+        read_the_signs(query_up_factor, ("replica", "tensor")),
         lax.all_gather(output_down_factor, ("replica", "tensor"), axis=1, tiled=True),
     )
     query_weight_slice = lax.dynamic_slice_in_dim(

time: 285 us -> 242 us (0.85)
  waiting for transfers between devices: 183 us -> 123 us
  starting transfers between devices: 0.15 us -> 8.91 us
  local copies, waits for them, and re-layouts: 28.7 us -> 36.4 us
    all_gather x1, waiting for transfers between devices: 54.9 us -> 0.01 us  [shards(): lax.all_gather(query_down_factor, ('replica', 'tensor'), axis=1, tiled=True)]
    all_gather x1, waiting for transfers between devices: 54.7 us -> 0.02 us  [shards(): lax.all_gather(output_down_factor, ('replica', 'tensor'), axis=1, tiled=T...]
    all_gather x1, waiting for transfers between devices: 15.2 us -> 55.2 us  [shards(): lax.all_gather(output_up_factor, ('replica', 'tensor'), axis=1, tiled=True)]
    ppermute x0 -> x5, waiting for transfers between devices: none -> 31 us  [read_the_signs(): right_arr = ppermute(small, mesh_dim, placed)]
    all_gather x1 -> x0, waiting for transfers between devices: 19.6 us -> none  [shards(): lax.all_gather(query_up_factor, ('replica', 'tensor'), axis=1, tiled=True)]
    ppermute x0 -> x5, starting transfers between devices: none -> 8.79 us  [read_the_signs(): right_arr = ppermute(small, mesh_dim, placed)]
    unnamed x13 -> x27, local copies, waits for them, and re-layouts: 21 us -> 27.7 us
  transfers between devices with their start and end apart: 5 -> 9, of which waited for: 5 -> 5; matrix products, arithmetic and copies ran while one was open for 27% -> 35% of each run, Pallas kernels for 0% -> 0%
where the time goes in v1:
time: 242 us; the launch traced here: 241 us
  waiting for transfers between devices  123 us (51%)
  matrix products  53.6 us (22%)
  local copies, waits for them, and re-layouts  36.4 us (15%)
  between operations  13.6 us (6%)
  starting transfers between devices  8.91 us (4%)
  other arithmetic  5.44 us (2%)
    all_gather x1, waiting for transfers between devices, shards(): lax.all_gather(output_up_factor, ('replica', 'tensor'), axis=1, tiled=True)  55.2 us
    reduce_scatter x1, waiting for transfers between devices, shards(): lax.psum_scatter(partial_all.astype(jnp.bfloat16), 'tensor', scatter_dime...  35.8 us
    ppermute x5, waiting for transfers between devices, read_the_signs(): right_arr = ppermute(small, mesh_dim, placed)  31 us
    unnamed x27, local copies, waits for them, and re-layouts  27.7 us
    dot_general x1, matrix products, shards(): jnp.dot(heads_stacked, output_merged_weight, preferred_element_type=jnp.f...  12 us
    dot_general x1, matrix products, rank_contraction(): lax.dot_general(left_factor, right_factor, (((0,), (0,)), ((), ())), pref...  11.8 us
    dot_general x1, matrix products, shards(): jnp.dot(normed_all, query_merged_weight, preferred_element_type=jnp.float32)  9.1 us
    ppermute x5, starting transfers between devices, read_the_signs(): right_arr = ppermute(small, mesh_dim, placed)  8.79 us
  transfers between devices with their start and end apart: 9, of which 5 were waited for; matrix products, arithmetic and copies ran while one was open for 35% of the time, Pallas kernels for 0%

profile of v1, /device:TPU:0, one launch (start us, length us, event | category | flops | bytes accessed | tf_op | source)
XLA Modules:
  0.0 241.3 jit_solution(6305287586013553664)
XLA Ops:
  6.5 0.7 all-gather.4.cloned.1.call-update
  7.3 0.7 all-gather.6.cloned.1.call-update
  8.1 6.5 %collective-permute-start = (bf16[64,256]{1,0:T(8,128)(2,1)}, bf16[64,256]{1,0:T(8,128)(2,1)S(1)}, u32[]{:S(2)}, u32[]{:S(2)}) collective-permute-start(bf16[64,256]{1,0:T(8,128)(2,1)} %param.18), channel_id=1, source_target_pairs={{0,31},{1,0},{2,1},{3,2},{4,3},{5,4},{6,5},{7,6},{8,7},{9,8},{10,9... | collective-permute-start | bytes 98312 | tf_op jit(solution)/shard_map/ppermute | solution.py:24
  14.6 0.7 convert_element_type.109
  15.3 1.5 fusion.6
  16.8 0.7 add_convert_fusion.5
  17.5 6.5 %copy.40 = bf16[256,8192]{1,0:T(8,128)(2,1)} copy(bf16[256,8192]{0,1:T(8,128)(2,1)} %bitcast.116) | data formatting | bytes 8388608 | tf_op jit(solution)/shard_map/reshape.133
  24.0 0.3 fusion.8
  24.3 4.0 %convolution_bitcast_fusion = f32[4,16,1,2,128]{4,1,3,0,2:T(8,128)S(1)} fusion(bf16[2,128,8192,1]{2,1,0,3:T(8,128)(2,1)} %bitcast.117, bf16[4,16,8192]{2,1,0:T(8,128)(2,1)S(1)} %fusion.8), kind=kOutput, calls=%fused_computation.23 | convolution fusion | flops 268435456 | bytes 5308416 | tf_op jit(solution)/shard_map/dot_general | solution.py:174
  28.4 1.2 collective-permute-start.1
  30.1 2.6 %collective-permute-done.1 = bf16[64,512]{1,0:T(8,128)(2,1)S(1)} collective-permute-done((bf16[64,512]{1,0:T(8,128)(2,1)S(1)}, bf16[64,512]{1,0:T(8,128)(2,1)S(1)}, u32[]{:S(2)}, u32[]{:S(2)}) %collective-permute-start.1) | collective-permute-done | bytes 65568 | tf_op jit(solution)/shard_map/ppermute | solution.py:24
  32.8 0.6 collective-permute-start.2
  33.5 20.9 %copy.24 = bf16[8192,1024]{0,1:T(8,128)(2,1)} copy(bf16[8192,1024]{1,0:T(8,128)(2,1)} %param.14) | data formatting | bytes 33554432 | tf_op args[2]
  54.5 0.6 constant_dynamic-update-slice_fusion.4
  55.1 0.5 collective-permute-start.3
  55.6 0.6 constant_dynamic-update-slice_fusion.3
  56.3 0.7 constant_dynamic-update-slice_fusion.2
  56.9 0.7 constant_dynamic-update-slice_fusion.1
  57.6 7.8 %collective-permute-done.3 = bf16[64,2048]{1,0:T(8,128)(2,1)S(1)} collective-permute-done((bf16[64,2048]{1,0:T(8,128)(2,1)S(1)}, bf16[64,2048]{1,0:T(8,128)(2,1)S(1)}, u32[]{:S(2)}, u32[]{:S(2)}) %collective-permute-start.3) | collective-permute-done | bytes 262176 | tf_op jit(solution)/shard_map/ppermute | solution.py:24
  65.4 0.8 constant_dynamic-update-slice_fusion
  66.5 20.6 %collective-permute-done.4 = bf16[64,4096]{1,0:T(8,128)(2,1)S(1)} collective-permute-done((bf16[64,4096]{1,0:T(8,128)(2,1)S(1)}, bf16[64,4096]{1,0:T(8,128)(2,1)S(1)}, u32[]{:S(2)}, u32[]{:S(2)}) %collective-permute-start.4) | collective-permute-done | bytes 524320 | tf_op jit(solution)/shard_map/ppermute | solution.py:24
  87.1 0.8 constant_dynamic-update-slice_fusion.11
  87.9 0.6 constant_dynamic-update-slice_fusion.10
  88.5 0.6 constant_dynamic-update-slice_fusion.9
  89.1 0.6 constant_dynamic-update-slice_fusion.8
  89.8 0.7 constant_dynamic-update-slice_fusion.7
  90.4 0.7 constant_dynamic-update-slice_fusion.6
  91.2 0.9 constant_dynamic-update-slice_fusion.5
  92.0 11.8 %fusion = bf16[8192,1024]{0,1:T(8,128)(2,1)} fusion(bf16[8192,1024]{0,1:T(8,128)(2,1)} %copy.24, bf16[64,8192]{1,0:T(8,128)(2,1)} %all-gather.4.cloned.1.call-done, bf16[64,16384]{1,0:T(8,128)(2,1)} %constant_dynamic-update-slice_fusion.5, s32[]{:T(128)S(6)} %dynamic_slice.11), kind=kOutput, calls=%fused_computation.1 | convolution fusion | flops 1107296256 | bytes 34734084 | tf_op jit(solution)/shard_map/dot_general | solution.py:94
  103.9 9.1 %fusion.72 = f32[64,8,128]{2,0,1:T(8,128)S(1)} fusion(bf16[64,8192,1]{1,0,2:T(8,128)(2,1)} %bitcast.115, bf16[8,128,8192]{2,1,0:T(8,128)(2,1)} %bitcast.106), kind=kOutput, calls=%fused_computation.142 | convolution fusion | flops 1073741824 | bytes 18087936 | tf_op jit(solution)/shard_map/dot_general | solution.py:170
  113.1 0.4 maximum_bitcast_fusion
  113.9 1.3 fusion.71
  115.2 2.0 fusion.69
  117.4 1.3 fusion.67
  118.7 0.2 fusion.18
  118.9 0.7 fusion.16
  120.0 2.9 %fusion.22 = f32[16,8,128]{2,1,0:T(8,128)S(1)} fusion(bf16[16,1024,128]{2,1,0:T(8,128)(2,1)} %bitcast.111, f32[16,8,1024]{2,1,0:T(8,128)S(1)} %copy-done.3, f32[16,8]{1,0:T(8,128)S(1)} %add.119, f32[16,8]{1,0:T(8,128)S(1)} %max.31), kind=kOutput, calls=%fused_computation.45 | convolution fusion | flops 33947648 | bytes 4785152 | tf_op jit(solution)/shard_map/ngp,npd->ngd/dot_general | solution.py:84
  122.9 0.2 fusion.13
  123.2 0.2 fusion.20
  123.4 2.9 %fusion.23 = f32[16,8,128]{2,1,0:T(8,128)S(1)} fusion(bf16[16,1024,128]{2,1,0:T(8,128)(2,1)} %bitcast.112, f32[16,8,1024]{2,1,0:T(8,128)S(1)} %get-tuple-element.32, f32[16,8]{1,0:T(8,128)S(1)} %add.121, f32[16,8]{1,0:T(8,128)S(1)} %max.32), kind=kOutput, calls=%fused_computation.46 | convolution fusion | flops 33947648 | bytes 4785152 | tf_op jit(solution)/shard_map/ngp,npd->ngd/dot_general | solution.py:84
  126.4 0.2 fusion.14
  126.8 3.6 %fusion.65 = (f32[16,8]{1,0:T(8,128)S(1)}, f32[16,8,1024]{2,1,0:T(8,128)S(1)}) fusion(bf16[16,8,128]{2,1,0:T(8,128)(2,1)S(1)} %bitcast.121, bf16[16,1024,128]{2,1,0:T(8,128)(2,1)} %bitcast.107, pred[16,1024]{1,0:T(8,128)(4,1)S(1)} %iota_compare_fusion), kind=kOutput, calls=%fused_computation.135 | convolution fusion | flops 33947520 | bytes 4768256 | tf_op jit(solution)/shard_map/ngd,npd->ngp/dot_general | solution.py:65
  130.5 0.2 fusion.21
  130.8 0.7 fusion.24
  131.5 0.2 fusion.15
  131.8 55.2 %all-gather.8.cloned.1.call-done = bf16[64,8192]{1,0:T(8,128)(2,1)} async-done(((bf16[64,256]{1,0:T(8,128)(2,1)}), bf16[64,8192]{1,0:T(8,128)(2,1)}) %all-gather.8.cloned.1.call-update) | async-done | bytes 1048592 | tf_op jit(solution)/shard_map/all_gather | solution.py:125
  187.0 12.0 %fusion.5 = bf16[64,8192]{1,0:T(8,128)(2,1)} fusion(bf16[64,1024]{1,0:T(8,128)(2,1)S(1)} %bitcast.130, bf16[1024,8192]{1,0:T(8,128)(2,1)} %param.16, bf16[64,8192]{1,0:T(8,128)(2,1)} %all-gather.8.cloned.1.call-done, bf16[64,8192]{1,0:T(8,128)(2,1)} %all-gather.6.cloned.1.call-done, s32[]{:T(128)S(6)} %select_n.34), kind=kOutput, calls=%fused_computation.6 | convolution fusion | flops 2181562368 | bytes 19136516 | tf_op jit(solution)/shard_map/dot_general | solution.py:267
  199.0 35.8 %reduce-scatter.2.cloned.1.call-done = bf16[64,1024]{1,0:T(8,128)(2,1)} async-done(((bf16[64,8192]{1,0:T(8,128)(2,1)}), bf16[64,1024]{1,0:T(8,128)(2,1)}) %reduce-scatter.2.cloned.1.call-update) | async-done | bytes 131088 | tf_op jit(solution)/shard_map/reduce_scatter | solution.py:268
  (77 shorter events, 2.6 us)
Async XLA Ops:
  6.5 85.5 %all-gather.4.cloned.1.call-start = ((), (), s32[]{:S(2)}) async-start(), calls=%async_computation.1 | async-start | bytes 1081344 | tf_op jit(solution)/shard_map/all_gather | solution.py:124
  7.3 124.5 %all-gather.6.cloned.1.call-start = ((), (), s32[]{:S(2)}) async-start(), calls=%async_computation.2 | async-start | bytes 1081344 | tf_op jit(solution)/shard_map/all_gather | solution.py:127
  8.0 178.9 %all-gather.8.cloned.1.call-start = ((), (), s32[]{:S(2)}) async-start(), calls=%async_computation.3 | async-start | bytes 1081344 | tf_op jit(solution)/shard_map/all_gather | solution.py:125
  8.1 20.3 %collective-permute-start = (bf16[64,256]{1,0:T(8,128)(2,1)}, bf16[64,256]{1,0:T(8,128)(2,1)S(1)}, u32[]{:S(2)}, u32[]{:S(2)}) collective-permute-start(bf16[64,256]{1,0:T(8,128)(2,1)} %param.18), channel_id=1, source_target_pairs={{0,31},{1,0},{2,1},{3,2},{4,3},{5,4},{6,5},{7,6},{8,7},{9,8},{10,9... | collective-permute-start | bytes 98312 | tf_op jit(solution)/shard_map/ppermute | solution.py:24
  14.5 220.2 %reduce-scatter.2.cloned.1.call-start = ((), (), s32[]{:S(2)}) async-start(), calls=%async_computation.4 | async-start | bytes 1179648 | tf_op jit(solution)/shard_map/reduce_scatter | solution.py:268
  17.5 6.5 %copy-start.5 = (bf16[4,16,8192]{2,1,0:T(8,128)(2,1)S(1)}, bf16[4,16,8192]{2,1,0:T(8,128)(2,1)}, u32[]{:S(2)}) copy-start(bf16[4,16,8192]{2,1,0:T(8,128)(2,1)} %param.12) | copy-start | bytes 3145732
  24.3 8.5 %copy-start.4 = (bf16[4,16,8192]{2,1,0:T(8,128)(2,1)}, bf16[4,16,8192]{2,1,0:T(8,128)(2,1)S(1)}, u32[]{:S(2)}) copy-start(bf16[4,16,8192]{2,1,0:T(8,128)(2,1)S(1)} %fusion.8) | copy-start | bytes 3145732
  24.3 4.1 %copy-start.6 = (bf16[64,256]{1,0:T(8,128)(2,1)S(1)}, bf16[64,256]{1,0:T(8,128)(2,1)}, u32[]{:S(2)}) copy-start(bf16[64,256]{1,0:T(8,128)(2,1)} %param.18) | copy-start | bytes 98308
  24.3 5.6 %copy-start.7 = (s32[16]{0:T(128)S(1)}, s32[16]{0:T(128)}, u32[]{:S(2)}) copy-start(s32[16]{0:T(128)} %param.23) | copy-start | bytes 196
  28.4 4.3 %collective-permute-start.1 = (bf16[64,512]{1,0:T(8,128)(2,1)S(1)}, bf16[64,512]{1,0:T(8,128)(2,1)S(1)}, u32[]{:S(2)}, u32[]{:S(2)}) collective-permute-start(bf16[64,512]{1,0:T(8,128)(2,1)S(1)} %pad_maximum_fusion.3), channel_id=1, source_target_pairs={{0,30},{1,31},{2,0},{3,1},{4,2},{5,3},{6,4},{7,5},{8,6},{9,7},{10,... | collective-permute-start | bytes 196616 | tf_op jit(solution)/shard_map/ppermute | solution.py:24
  32.8 22.3 %collective-permute-start.2 = (bf16[64,1024]{1,0:T(8,128)(2,1)S(1)}, bf16[64,1024]{1,0:T(8,128)(2,1)S(1)}, u32[]{:S(2)}, u32[]{:S(2)}) collective-permute-start(bf16[64,1024]{1,0:T(8,128)(2,1)S(1)} %pad_maximum_fusion.1), channel_id=1, source_target_pairs={{0,28},{1,29},{2,30},{3,31},{4,0},{5,1},{6,2},{7,3},{8,4},{9,5},{1... | collective-permute-start | bytes 393224 | tf_op jit(solution)/shard_map/ppermute | solution.py:24
  55.1 10.3 %collective-permute-start.3 = (bf16[64,2048]{1,0:T(8,128)(2,1)S(1)}, bf16[64,2048]{1,0:T(8,128)(2,1)S(1)}, u32[]{:S(2)}, u32[]{:S(2)}) collective-permute-start(bf16[64,2048]{1,0:T(8,128)(2,1)S(1)} %pad_maximum_fusion), channel_id=1, source_target_pairs={{0,24},{1,25},{2,26},{3,27},{4,28},{5,29},{6,30},{7,31},{8,0},{9,1... | collective-permute-start | bytes 786440 | tf_op jit(solution)/shard_map/ppermute | solution.py:24
  66.2 20.9 %collective-permute-start.4 = (bf16[64,4096]{1,0:T(8,128)(2,1)S(1)}, bf16[64,4096]{1,0:T(8,128)(2,1)S(1)}, u32[]{:S(2)}, u32[]{:S(2)}) collective-permute-start(bf16[64,4096]{1,0:T(8,128)(2,1)S(1)} %get-tuple-element.7), channel_id=1, source_target_pairs={{0,16},{1,17},{2,18},{3,19},{4,20},{5,21},{6,22},{7,23},{8,24},{9,... | collective-permute-start | bytes 1572872 | tf_op jit(solution)/shard_map/ppermute | solution.py:24
  103.9 10.1 %copy-start = (bf16[2,8,1024,128]{3,2,1,0:T(8,128)(2,1)S(1)}, bf16[2,8,1024,128]{3,2,1,0:T(8,128)(2,1)}, u32[]{:S(2)}) copy-start(bf16[2,8,1024,128]{3,2,1,0:T(8,128)(2,1)} %param.21) | copy-start | bytes 12582916
  115.2 3.7 %copy-start.1 = (bf16[2,8,1024,128]{3,2,1,0:T(8,128)(2,1)S(1)}, bf16[2,8,1024,128]{3,2,1,0:T(8,128)(2,1)}, u32[]{:S(2)}) copy-start(bf16[2,8,1024,128]{3,2,1,0:T(8,128)(2,1)} %param.22) | copy-start | bytes 12582916
  118.7 1.1 copy-start.3
  126.6 4.1 %copy-start.2 = (bf16[2,8,1024,128]{3,2,1,0:T(8,128)(2,1)S(1)}, bf16[2,8,1024,128]{3,2,1,0:T(8,128)(2,1)}, u32[]{:S(2)}) copy-start(bf16[2,8,1024,128]{3,2,1,0:T(8,128)(2,1)} %param.22) | copy-start | bytes 12582916
Sparse Core Ops, SparseCore 0:
  10.2 56.3 all-gather.3
  69.4 62.2 all-gather.5
  134.6 52.2 all-gather.7
  199.1 35.6 reduce-scatter.1
